TPU v7x, 128 devices: a whole 4x4x4 slice. The times are simulated.
128 devices in a mesh: dp: 32 (over x, y, z_lo), seq: 4 (over z_hi, core).
Axes of the slice: x: 4, y: 4, z: 4 (z_hi: 2, z_lo: 2; z = z_hi * 2 + z_lo), core: 2. Of those that a mesh axis runs over, the one named last changes fastest.
Arguments:
- qkv: bfloat16 [64, 1024, 4608], P('dp', 'seq'), may hold values from -20.4 to 20.4
- gate: float32 [64, 3072], P('dp'), may hold values from 0.5 to 2.5
- cotangent: bfloat16 [64, 1024, 3072], P('dp', 'seq'), may hold values from -6 to 6
- out_weight: bfloat16 [1536, 3072], replicated, may hold values from -0.15625 to 0.15625
- clip_lengths: int32 [64], replicated, may hold values from 1 to 768, as said below
- text_lengths: int32 [64], replicated, may hold values from 1 to 256, as said below
- plan: int32 [32], replicated, may hold values from 0 to 31, as said below
Outputs:
- mixed: bfloat16 [64, 1024, 3072], P('dp', 'seq')
- gate_grad: float32 [64, 3072], P('dp')
- weight_grad: float32 [1536, 3072], P(None, ('dp', 'seq'))
- qkv_grad: bfloat16 [64, 1024, 4608], P('dp', 'seq')
Inputs may be any that keep to these rules, and one draw needn't show every extreme that they name: clip_lengths[c] counts the live video positions of source clip c = 2 g + s (group g, slot s); some clip has exactly 768. text_lengths[c] counts the live text positions of source clip c; some clip has exactly 256. plan is a permutation of 0 to 31: the second clip of group g becomes the second clip of group plan[g].
All inputs are finite; a program needn't handle non-finite values.
Results may differ from a plain program's by a relative error of at most 0.011.
Values may be sent and summed in bfloat16 or wider, within the bound.
No kernel may reach another device: no remote copies, remote signals or barrier semaphores. Data moves between devices by JAX's collectives and lax.ppermute only.
A program may use at most 128 MiB of HBM per device.

v0:
```python
import jax
import jax.numpy as jnp
from jax import lax
from jax.sharding import PartitionSpec as P

HD = 128
TXT = 256
BLOCK = 512
NEGATIVE = -1e30


def from_everyone(x, axis):
    copies = jnp.broadcast_to(x, (lax.axis_size(axis), *x.shape))
    return lax.all_to_all(copies, axis, split_axis=0, concat_axis=0, tiled=True)


def taken_together(x, axis):
    everything = from_everyone(x, axis)
    return jnp.sum(everything, axis=0)


def allowed_rows(offset, count, text_len, video_len):
    places = offset + jnp.arange(count, dtype=jnp.int32)
    return (places < text_len) | (places >= TXT) & (places < TXT + video_len)


def move_in(block_rows, inverse):
    groups = lax.axis_size("dp")
    portions = block_rows.reshape(groups, block_rows.shape[0] // groups, block_rows.shape[1])
    spread = lax.all_to_all(portions, "dp", split_axis=0, concat_axis=0, tiled=True)
    arranged = jnp.take(spread, inverse, axis=0)
    landed = lax.all_to_all(arranged, "dp", split_axis=0, concat_axis=0, tiled=True)
    return landed.reshape(block_rows.shape)


def move_out(block_rows, plan):
    groups = lax.axis_size("dp")
    portions = block_rows.reshape(groups, block_rows.shape[0] // groups, block_rows.shape[1])
    spread = lax.all_to_all(portions, "dp", split_axis=0, concat_axis=0, tiled=True)
    arranged = jnp.take(spread, plan, axis=0)
    landed = lax.all_to_all(arranged, "dp", split_axis=0, concat_axis=0, tiled=True)
    return landed.reshape(block_rows.shape)


def to_heads(tokens, seq_ways):
    clip_count, row_count, full_width = tokens.shape
    local_width = full_width // (3 * seq_ways)
    parted = tokens.reshape(clip_count, row_count, 3, seq_ways, local_width)
    exchanged = lax.all_to_all(parted, "seq", split_axis=3, concat_axis=1, tiled=True)
    return exchanged.reshape(clip_count, row_count * seq_ways, 3, local_width)


def block_scores(query_rows, key_rows, query_ok, key_ok, score_scale):
    scores = (
        jnp.einsum("qhd,khd->hqk", query_rows, key_rows, preferred_element_type=jnp.float32)
        * score_scale
    )
    live_pairs = query_ok[None, :, None] & key_ok[None, None, :]
    return (scores, live_pairs)


def attend(queries, keys_all, values_all, text_len, video_len, score_scale):
    seq_len, head_count, head_dim = queries.shape
    block_count = (TXT + video_len + BLOCK - 1) // BLOCK

    def query_step(query_block, built):
        results, log_totals = built
        offset = query_block * BLOCK
        query_rows = lax.dynamic_slice_in_dim(queries, offset, BLOCK, 0)
        query_ok = allowed_rows(offset, BLOCK, text_len, video_len)

        def scored(key_block):
            key_offset = key_block * BLOCK
            key_rows = lax.dynamic_slice_in_dim(keys_all, key_offset, BLOCK, 0)
            key_ok = allowed_rows(key_offset, BLOCK, text_len, video_len)
            scores, live_pairs = block_scores(query_rows, key_rows, query_ok, key_ok, score_scale)
            return (scores, live_pairs, key_offset)

        def stats_step(key_block, running):
            row_peak, row_total = running
            scores, live_pairs, key_offset = scored(key_block)
            masked = jnp.where(live_pairs, scores, NEGATIVE)
            new_peak = jnp.maximum(row_peak, jnp.max(masked, axis=-1))
            row_total = row_total * jnp.exp(row_peak - new_peak) + jnp.sum(
                jnp.exp(masked - new_peak[..., None]), axis=-1
            )
            return (new_peak, row_total)

        start_peak = jnp.full((head_count, BLOCK), NEGATIVE, jnp.float32)
        row_peak, row_total = lax.fori_loop(
            0, block_count, stats_step, (start_peak, jnp.zeros((head_count, BLOCK), jnp.float32))
        )
        log_total = row_peak + jnp.log(row_total)

        def value_step(key_block, partial_sums):
            scores, live_pairs, key_offset = scored(key_block)
            probs_low = jnp.exp(
                jnp.where(live_pairs, scores - log_total[..., None], NEGATIVE)
            ).astype(jnp.bfloat16)
            value_rows = lax.dynamic_slice_in_dim(values_all, key_offset, BLOCK, 0)
            return partial_sums + jnp.einsum(
                "hqk,khd->qhd", probs_low, value_rows, preferred_element_type=jnp.float32
            )

        partial_sums = lax.fori_loop(
            0, block_count, value_step, jnp.zeros((BLOCK, head_count, head_dim), jnp.float32)
        )
        results = lax.dynamic_update_slice_in_dim(
            results, partial_sums.astype(jnp.bfloat16), offset, 0
        )
        log_totals = lax.dynamic_update_slice_in_dim(log_totals, log_total, offset, 1)
        return (results, log_totals)

    initial = (
        jnp.zeros((seq_len, head_count, head_dim), jnp.bfloat16),
        jnp.zeros((head_count, seq_len), jnp.float32),
    )
    return lax.fori_loop(0, block_count, query_step, initial)


def attend_back(
    queries, keys_all, values_all, results, d_results, log_totals, text_len, video_len, score_scale
):
    seq_len, head_count, head_dim = queries.shape
    block_count = (TXT + video_len + BLOCK - 1) // BLOCK
    row_dots_all = jnp.einsum("qhd,qhd->hq", d_results, results, preferred_element_type=jnp.float32)

    def query_step(query_block, gradients):
        grad_q, grad_k, grad_v = gradients
        offset = query_block * BLOCK
        query_rows = lax.dynamic_slice_in_dim(queries, offset, BLOCK, 0)
        d_rows = lax.dynamic_slice_in_dim(d_results, offset, BLOCK, 0)
        query_ok = allowed_rows(offset, BLOCK, text_len, video_len)
        log_total = lax.dynamic_slice_in_dim(log_totals, offset, BLOCK, 1)
        row_dots = lax.dynamic_slice_in_dim(row_dots_all, offset, BLOCK, 1)

        def key_step(key_block, inner_state):
            q_sums, grad_k, grad_v = inner_state
            key_offset = key_block * BLOCK
            key_rows = lax.dynamic_slice_in_dim(keys_all, key_offset, BLOCK, 0)
            value_rows = lax.dynamic_slice_in_dim(values_all, key_offset, BLOCK, 0)
            key_ok = allowed_rows(key_offset, BLOCK, text_len, video_len)
            scores, live_pairs = block_scores(query_rows, key_rows, query_ok, key_ok, score_scale)
            probabilities = jnp.exp(jnp.where(live_pairs, scores - log_total[..., None], NEGATIVE))
            probs_low = probabilities.astype(jnp.bfloat16)
            d_probs = jnp.einsum(
                "qhd,khd->hqk", d_rows, value_rows, preferred_element_type=jnp.float32
            )
            d_scores = (probabilities * (d_probs - row_dots[..., None])).astype(jnp.bfloat16)
            q_sums = q_sums + jnp.einsum(
                "hqk,khd->qhd", d_scores, key_rows, preferred_element_type=jnp.float32
            )
            k_part = jnp.einsum(
                "hqk,qhd->khd", d_scores, query_rows, preferred_element_type=jnp.float32
            )
            v_part = jnp.einsum(
                "hqk,qhd->khd", probs_low, d_rows, preferred_element_type=jnp.float32
            )
            grad_k = lax.dynamic_update_slice_in_dim(
                grad_k,
                lax.dynamic_slice_in_dim(grad_k, key_offset, BLOCK, 0) + k_part,
                key_offset,
                0,
            )
            grad_v = lax.dynamic_update_slice_in_dim(
                grad_v,
                lax.dynamic_slice_in_dim(grad_v, key_offset, BLOCK, 0) + v_part,
                key_offset,
                0,
            )
            return (q_sums, grad_k, grad_v)

        q_start = jnp.zeros((BLOCK, head_count, head_dim), jnp.float32)
        q_sums, grad_k, grad_v = lax.fori_loop(0, block_count, key_step, (q_start, grad_k, grad_v))
        grad_q = lax.dynamic_update_slice_in_dim(grad_q, q_sums, offset, 0)
        return (grad_q, grad_k, grad_v)

    zero_grad = jnp.zeros((seq_len, head_count, head_dim), jnp.float32)
    grad_q, grad_k, grad_v = lax.fori_loop(
        0, block_count, query_step, (zero_grad, zero_grad, zero_grad)
    )
    return (
        (grad_q * score_scale).astype(jnp.bfloat16),
        (grad_k * score_scale).astype(jnp.bfloat16),
        grad_v.astype(jnp.bfloat16),
    )


def body(qkv, gate, cotangent, out_weight, clip_lengths, text_lengths, plan):
    groups = lax.axis_size("dp")
    seq_ways = lax.axis_size("seq")
    group_index = lax.axis_index("dp")
    seq_index = lax.axis_index("seq")
    ordinal = jnp.arange(groups, dtype=jnp.int32)
    inverse = jnp.sum(jnp.where(plan[None, :] == ordinal[:, None], ordinal[None, :], 0), axis=1)
    home_clip = 2 * group_index
    head_width = out_weight.shape[0]
    local_width = head_width // seq_ways
    head_count = local_width // HD
    row_count = cotangent.shape[1]
    score_scale = HD ** (-0.5)
    arrived = move_in(qkv[1], inverse)
    working = jnp.stack([qkv[0], arrived])
    clip_ids = (home_clip, 2 * inverse[group_index] + 1)
    spread_heads = to_heads(working, seq_ways)
    seq_len = spread_heads.shape[1]
    video_lens = [clip_lengths[clip_id] for clip_id in clip_ids]
    text_lens = [text_lengths[clip_id] for clip_id in clip_ids]
    sections = []
    result_list = []
    log_list = []
    for slot_index in range(2):
        triple = [
            spread_heads[slot_index, :, member].reshape(seq_len, head_count, HD)
            for member in range(3)
        ]
        results, log_totals = attend(
            triple[0],
            triple[1],
            triple[2],
            text_lens[slot_index],
            video_lens[slot_index],
            score_scale,
        )
        sections.append(triple)
        result_list.append(results)
        log_list.append(log_totals)
    attn_heads = jnp.stack(result_list).reshape(2, seq_len, 1, local_width)
    attn_back = lax.all_to_all(attn_heads, "seq", split_axis=1, concat_axis=2, tiled=True).reshape(
        2, row_count, head_width
    )
    outputs = jnp.einsum("crh,hd->crd", attn_back, out_weight, preferred_element_type=jnp.float32)
    mixed = (gate[:, None, :] * outputs).astype(jnp.bfloat16)
    gate_grad = taken_together(jnp.sum(cotangent.astype(jnp.float32) * outputs, axis=1), "seq")
    scaled = (cotangent.astype(jnp.float32) * gate[:, None, :]).astype(jnp.bfloat16)
    weight_rows = lax.dynamic_slice_in_dim(out_weight, seq_index * local_width, local_width, 0)
    flat_heads = attn_heads.reshape(2, seq_len, local_width)
    portion = lax.all_gather(scaled, "seq", axis=1, tiled=True)
    weight_part = jnp.einsum("cnh,cnd->hd", flat_heads, portion, preferred_element_type=jnp.float32)
    grad_rows = jnp.einsum(
        "cnd,hd->cnh", portion, weight_rows, preferred_element_type=jnp.float32
    ).astype(jnp.bfloat16)
    d_heads, weight_part = (grad_rows, weight_part)
    summed = lax.psum_scatter(weight_part, "dp", scatter_dimension=1, tiled=True)
    weight_grad = lax.all_to_all(summed, "seq", split_axis=1, concat_axis=0, tiled=True)
    grad_list = []
    for slot_index in range(2):
        triple = sections[slot_index]
        d_rows = d_heads[slot_index].reshape(seq_len, head_count, HD)
        grad_parts = attend_back(
            triple[0],
            triple[1],
            triple[2],
            result_list[slot_index],
            d_rows,
            log_list[slot_index],
            text_lens[slot_index],
            video_lens[slot_index],
            score_scale,
        )
        grad_list.append(
            jnp.stack([grad_part.reshape(seq_len, local_width) for grad_part in grad_parts], axis=1)
        )
    grad_heads = jnp.stack(grad_list).reshape(2, seq_len, 3, 1, local_width)
    grad_tokens = lax.all_to_all(
        grad_heads, "seq", split_axis=1, concat_axis=3, tiled=True
    ).reshape(2, row_count, 3 * head_width)
    grad_tokens = jnp.stack([grad_tokens[0], move_out(grad_tokens[1], plan)])
    return (mixed, gate_grad, weight_grad, grad_tokens)


def solution(mesh):
    in_specs = (P("dp", "seq", None), P("dp", None), P("dp", "seq", None), P(), P(), P(), P())
    out_specs = (P("dp", "seq", None), P("dp", None), P(None, ("dp", "seq")), P("dp", "seq", None))
    return jax.shard_map(body, mesh=mesh, in_specs=in_specs, out_specs=out_specs, check_vma=False)
```

profile of v0, /device:TPU:1, one launch (start us, length us, event | category | flops | bytes accessed | tf_op | source)
XLA Modules:
  0.0 709.6 jit_solution(8524687649885798854)
XLA Ops:
  12.0 9.3 %all-to-all-start = ((bf16[32,8,4608]{2,1,0:T(8,128)(2,1)}), bf16[32,8,4608]{2,1,0:T(8,128)(2,1)S(1)}, u32[]{:S(2)}, u32[]{:S(2)}) async-start(bf16[32,8,4608]{2,1,0:T(8,128)(2,1)} %get-tuple-element.2898), calls=%async_computation | async-start | bytes 4718592 | tf_op jit(solution)/shard_map/all_to_all | solution.py:30
  21.5 30.6 %all-to-all-done = bf16[32,8,4608]{2,1,0:T(8,128)(2,1)S(1)} async-done(((bf16[32,8,4608]{2,1,0:T(8,128)(2,1)}), bf16[32,8,4608]{2,1,0:T(8,128)(2,1)S(1)}, u32[]{:S(2)}, u32[]{:S(2)}) %all-to-all-start) | async-done | bytes 2359328 | tf_op jit(solution)/shard_map/all_to_all | solution.py:30
  66.1 25.9 %all-to-all-done.1 = bf16[32,8,4608]{2,1,0:T(8,128)(2,1)S(1)} async-done(((bf16[32,8,4608]{2,1,0:T(8,128)(2,1)}), bf16[32,8,4608]{2,1,0:T(8,128)(2,1)S(1)}, u32[]{:S(2)}, u32[]{:S(2)}) %all-to-all-start.1) | async-done | bytes 2359328 | tf_op jit(solution)/shard_map/all_to_all | solution.py:32
  94.1 5.5 copy.325
  104.3 8.3 %all-to-all-start.2 = ((bf16[2,256,3,4,384]{1,4,2,0,3:T(8,128)(2,1)}), bf16[2,256,3,4,384]{1,4,2,0,3:T(8,128)(2,1)}, u32[]{:S(2)}, u32[]{:S(2)}) async-start(bf16[2,256,3,4,384]{1,4,2,0,3:T(8,128)(2,1)} %copy.326), calls=%async_computation.2 | async-start | bytes 9437184 | tf_op jit(solution)/shard_map/all_to_all | solution.py:49
  117.0 49.8 %all-to-all-done.2 = bf16[2,256,3,4,384]{1,4,2,0,3:T(8,128)(2,1)} async-done(((bf16[2,256,3,4,384]{1,4,2,0,3:T(8,128)(2,1)}), bf16[2,256,3,4,384]{1,4,2,0,3:T(8,128)(2,1)}, u32[]{:S(2)}, u32[]{:S(2)}) %all-to-all-start.2) | async-done | bytes 4718624 | tf_op jit(solution)/shard_map/all_to_all | solution.py:49
  166.9 6.6 copy.327
  181.5 25.5 %while.235 = (s32[]{:T(128)}, bf16[1024,3,128]{0,2,1:T(8,128)(2,1)S(1)}, f32[3,1024]{1,0:T(4,128)}, s32[]{:T(128)}, bf16[1024,3,128]{2,0,1:T(8,128)(2,1)}, /*ind...) while((s32[]{:T(128)}, ...), condition=%wide.region_16.18_spmd, body=%wide.region_9.17_spmd.sunk | while | flops 613564928 | bytes 14026645 | solution.py:118
  187.8 6.3 while.243
  200.5 6.3 while.243
  218.5 8.6 %while.232 = (s32[]{:T(128)}, bf16[1024,3,128]{0,2,1:T(8,128)(2,1)}, f32[3,1024]{1,0:T(4,128)}, s32[]{:T(128)}, bf16[1024,3,128]{2,0,1:T(8,128)(2,1)}, /*index=5...) while((s32[]{:T(128)}, bf16[1024,3,128]{0,2,1:T(8,128)(2,1)}, ...), condition=%wide.region_8.10_spmd, body=%wide.region_1.9_spmd.sunk | while | flops 613564928 | bytes 14026645 | solution.py:118
  234.3 24.0 %all_to_all.89 = bf16[2,1024,1,384]{3,0,2,1:T(2,128)(2,1)S(1)} all-to-all(bf16[2,1024,1,384]{3,0,2,1:T(2,128)(2,1)S(1)} %copy.338), channel_id=1, replica_groups=mesh['dp'=32,'seq'=4] {'seq'}, dimensions={1} | all-to-all | bytes 3145728 | tf_op jit(solution)/shard_map/all_to_all | solution.py:229
  261.3 11.0 %fusion.166 = (f32[2,3072]{1,0:T(2,128)}, bf16[2,256,3072]{2,1,0:T(8,128)(2,1)}, bf16[2,256,3072]{2,1,0:T(8,128)(2,1)}) fusion(bf16[2,256,3072]{2,1,0:T(8,128)(2,1)} %param.31, f32[2,3072]{1,0:T(2,128)S(1)} %copy-done.29, bf16[2,256,1536]{2,1,0:T(8,128)(2,1)} %reshape.316, bf16[1536,3072]{1,0:T(8,128)(2,1)} %param.32), kind=kOutput, calls=%fused_computation.198 | convolution fusion | flops 4842842112 | bytes 20496384 | tf_op jit(solution)/shard_map/crh,hd->crd/dot_general | solution.py:232
  279.3 76.6 %all-gather.2.cloned.1.call-done = bf16[2,1024,3072]{2,1,0:T(8,128)(2,1)} async-done(((bf16[2,256,3072]{2,1,0:T(8,128)(2,1)}), bf16[2,1024,3072]{2,1,0:T(8,128)(2,1)}) %all-gather.2.cloned.1.call-update) | async-done | bytes 12582928 | tf_op jit(solution)/shard_map/all_gather | solution.py:238
  355.8 13.5 %fusion.171 = bf16[2,1024,384]{1,2,0:T(8,128)(2,1)S(1)} fusion(bf16[2,1024,3072]{2,1,0:T(8,128)(2,1)} %all-gather.2.cloned.1.call-done, bf16[1536,3072]{1,0:T(8,128)(2,1)} %param.32, s32[]{:T(128)S(6)} %select_n.154), kind=kOutput, calls=%fused_computation.213 | convolution fusion | flops 4832624640 | bytes 16515076 | tf_op jit(solution)/shard_map/cnd,hd->cnh/dot_general | solution.py:240
  374.0 36.1 %while.239 = (s32[]{:T(128)}, f32[1024,3,128]{0,2,1:T(8,128)}, f32[1024,3,128]{2,0,1:T(8,128)S(1)}, f32[1024,3,128]{2,0,1:T(8,128)}, s32[]{:T(128)}, /*index=5*/...) while((s32[]{:T(128)}, f32[1024,3,128]{0,2,1:T(8,128)}, ...), condition=%wide.region_27.29_spmd, body=%wide.region_24.28_spmd.sunk | while | flops 1015355392 | bytes 44485396 | solution.py:179
  378.0 13.3 %while.245 = (s32[]{:T(128)}, f32[512,3,128]{0,2,1:T(8,128)S(1)}, f32[1024,3,128]{2,0,1:T(8,128)S(1)}, f32[1024,3,128]{2,0,1:T(8,128)}, s32[]{:T(128)}, /*index=...) while((s32[]{:T(128)}, f32[512,3,128]{0,2,1:T(8,128)S(1)}, ...), condition=%wide.region_26.27_spmd.clone.clone, body=%wide.region_25.26_spmd.clone.clone.sunk | while | flops 1015355392 | bytes 39741808 | solution.py:174
  395.9 13.2 %while.245 = (s32[]{:T(128)}, f32[512,3,128]{0,2,1:T(8,128)S(1)}, f32[1024,3,128]{2,0,1:T(8,128)S(1)}, f32[1024,3,128]{2,0,1:T(8,128)}, s32[]{:T(128)}, /*index=...) while((s32[]{:T(128)}, f32[512,3,128]{0,2,1:T(8,128)S(1)}, ...), condition=%wide.region_26.27_spmd.clone.clone, body=%wide.region_25.26_spmd.clone.clone.sunk | while | flops 1015355392 | bytes 39741808 | solution.py:174
  422.9 11.4 %while.237 = (s32[]{:T(128)}, f32[1024,3,128]{0,2,1:T(8,128)}, f32[1024,3,128]{2,0,1:T(8,128)S(1)}, f32[1024,3,128]{2,0,1:T(8,128)}, s32[]{:T(128)}, /*index=5*/...) while((s32[]{:T(128)}, f32[1024,3,128]{0,2,1:T(8,128)}, ...), condition=%wide.region_23.25_spmd, body=%wide.region_20.24_spmd.sunk | while | flops 1015355392 | bytes 44485404 | solution.py:179
  426.7 6.7 while.244
  444.6 12.6 %copy.362 = bf16[2,1024,3,1,384]{4,0,3,2,1:T(2,128)(2,1)} copy(bf16[2,1024,3,1,384]{1,4,2,0,3:T(8,128)(2,1)} %maximum_bitcast_fusion) | data formatting | bytes 9437184 | tf_op jit(solution)/shard_map/reshape | solution.py:264
  457.3 5.5 all-to-all-start.6
  462.8 11.1 %convolution_bitcast_fusion.4 = f32[384,3072]{0,1:T(8,128)} fusion(bf16[2,1024,3072]{2,1,0:T(8,128)(2,1)} %all-gather.2.cloned.1.call-done, bf16[1,1024,384]{2,1,0:T(8,128)(2,1)S(1)} %copy-done.22, bf16[1,1024,384]{2,1,0:T(8,128)(2,1)S(1)} %copy-done.23), kind=kOutput, calls=%fused_computation.204 | convolution fusion | flops 4832624640 | bytes 18874368 | tf_op jit(solution)/shard_map/cnh,cnd->hd/dot_general | solution.py:239
  473.9 96.9 %all-to-all-done.6 = bf16[2,1024,3,1,384]{4,0,3,2,1:T(2,128)(2,1)} async-done(((bf16[2,1024,3,1,384]{4,0,3,2,1:T(2,128)(2,1)}), bf16[2,1024,3,1,384]{4,0,3,2,1:T(2,128)(2,1)}, u32[]{:S(2)}, u32[]{:S(2)}) %all-to-all-start.6) | async-done | bytes 4718624 | tf_op jit(solution)/shard_map/all_to_all | solution.py:265
  579.9 14.0 %all-to-all-start.7 = ((bf16[32,8,4608]{2,1,0:T(8,128)(2,1)}), bf16[32,8,4608]{2,1,0:T(8,128)(2,1)S(1)}, u32[]{:S(2)}, u32[]{:S(2)}) async-start(bf16[32,8,4608]{2,1,0:T(8,128)(2,1)} %reshape_squeeze.39), calls=%async_computation.8 | async-start | bytes 4718592 | tf_op jit(solution)/shard_map/all_to_all | solution.py:39
  593.9 28.4 %all-to-all-done.7 = bf16[32,8,4608]{2,1,0:T(8,128)(2,1)S(1)} async-done(((bf16[32,8,4608]{2,1,0:T(8,128)(2,1)}), bf16[32,8,4608]{2,1,0:T(8,128)(2,1)S(1)}, u32[]{:S(2)}, u32[]{:S(2)}) %all-to-all-start.7) | async-done | bytes 2359328 | tf_op jit(solution)/shard_map/all_to_all | solution.py:39
  622.9 9.2 %all-to-all-start.4 = ((f32[4,2,3072]{2,1,0:T(2,128)}), f32[4,2,3072]{2,1,0:T(2,128)S(1)}, u32[]{:S(2)}, u32[]{:S(2)}) async-start(f32[4,2,3072]{2,1,0:T(2,128)} %broadcast_in_dim.133), calls=%async_computation.4 | async-start | bytes 196608 | tf_op jit(solution)/shard_map/all_to_all | solution.py:14
  638.2 6.1 all-to-all-start.8
  649.3 25.0 %all-to-all-done.8 = bf16[32,8,4608]{2,1,0:T(8,128)(2,1)S(1)} async-done(((bf16[32,8,4608]{2,1,0:T(8,128)(2,1)}), bf16[32,8,4608]{2,1,0:T(8,128)(2,1)S(1)}, u32[]{:S(2)}, u32[]{:S(2)}) %all-to-all-start.8) | async-done | bytes 2359328 | tf_op jit(solution)/shard_map/all_to_all | solution.py:41
  676.8 13.5 %all-to-all-start.5 = ((f32[384,4,24]{0,2,1:T(8,128)}), f32[384,4,24]{0,2,1:T(8,128)S(1)}, u32[]{:S(2)}, u32[]{:S(2)}) async-start(f32[384,4,24]{0,2,1:T(8,128)} %bitcast.308), calls=%async_computation.6 | async-start | bytes 294912 | tf_op jit(solution)/shard_map/all_to_all | solution.py:245
  690.3 5.0 pad_maximum_fusion.1
  695.3 6.6 copy.367
  (292 shorter events, 209.4 us)
Async XLA Ops:
  12.0 9.4 %copy-start.30 = (s32[32]{0:T(128)S(1)}, s32[32]{0:T(128)}, u32[]{:S(2)}) copy-start(s32[32]{0:T(128)} %param.35) | copy-start | bytes 388
  12.0 40.1 %all-to-all-start = ((bf16[32,8,4608]{2,1,0:T(8,128)(2,1)}), bf16[32,8,4608]{2,1,0:T(8,128)(2,1)S(1)}, u32[]{:S(2)}, u32[]{:S(2)}) async-start(bf16[32,8,4608]{2,1,0:T(8,128)(2,1)} %get-tuple-element.2898), calls=%async_computation | async-start | bytes 4718592 | tf_op jit(solution)/shard_map/all_to_all | solution.py:30
  57.6 34.4 %all-to-all-start.1 = ((bf16[32,8,4608]{2,1,0:T(8,128)(2,1)}), bf16[32,8,4608]{2,1,0:T(8,128)(2,1)S(1)}, u32[]{:S(2)}, u32[]{:S(2)}) async-start(bf16[32,8,4608]{2,1,0:T(8,128)(2,1)} %broadcast_select_fusion.1), calls=%async_computation.1 | async-start | bytes 4718592 | tf_op jit(solution)/shard_map/all_to_all | solution.py:32
  94.1 5.5 copy-start.10
  104.3 9.5 %copy-start.27 = (s32[64]{0:T(128)S(1)}, s32[64]{0:T(128)}, u32[]{:S(2)}) copy-start(s32[64]{0:T(128)} %param.34) | copy-start | bytes 772
  104.3 9.5 %copy-start.28 = (s32[64]{0:T(128)S(1)}, s32[64]{0:T(128)}, u32[]{:S(2)}) copy-start(s32[64]{0:T(128)} %param.33) | copy-start | bytes 772
  104.3 62.6 %all-to-all-start.2 = ((bf16[2,256,3,4,384]{1,4,2,0,3:T(8,128)(2,1)}), bf16[2,256,3,4,384]{1,4,2,0,3:T(8,128)(2,1)}, u32[]{:S(2)}, u32[]{:S(2)}) async-start(bf16[2,256,3,4,384]{1,4,2,0,3:T(8,128)(2,1)} %copy.326), calls=%async_computation.2 | async-start | bytes 9437184 | tf_op jit(solution)/shard_map/all_to_all | solution.py:49
  112.5 243.3 %all-gather.2.cloned.1.call-start = ((), (), s32[]{:S(2)}) async-start(), calls=%async_computation.10 | async-start | bytes 15728640 | tf_op jit(solution)/shard_map/all_gather | solution.py:238
  207.0 6.1 copy-start.6
  207.0 4.9 copy-start.16
  227.1 7.3 %copy-start = (bf16[1024,3,128]{2,0,1:T(8,128)(2,1)}, bf16[1024,3,128]{2,0,1:T(8,128)(2,1)S(1)}, u32[]{:S(2)}) copy-start(bf16[1024,3,128]{2,0,1:T(8,128)(2,1)S(1)} %get-tuple-element.4344) | copy-start | bytes 2359300
  259.8 1.5 copy-start.29
  272.3 4.6 copy-start.7
  273.4 4.7 copy-start.4
  370.4 2.3 copy-start.3
  414.3 5.0 copy-start.2
  414.3 5.0 copy-start.5
  420.2 2.7 copy-start.1
  436.9 3.3 copy-start.13
  438.6 1.9 copy-start.18
  438.6 1.9 copy-start.19
  438.6 2.1 copy-start.20
  457.3 5.5 copy-start.22
  457.3 5.5 copy-start.23
  457.3 113.5 %all-to-all-start.6 = ((bf16[2,1024,3,1,384]{4,0,3,2,1:T(2,128)(2,1)}), bf16[2,1024,3,1,384]{4,0,3,2,1:T(2,128)(2,1)}, u32[]{:S(2)}, u32[]{:S(2)}) async-start(bf16[2,1024,3,1,384]{4,0,3,2,1:T(2,128)(2,1)} %copy.362), calls=%async_computation.7 | async-start | bytes 9437184 | tf_op jit(solution)/shard_map/all_to_all | solution.py:265
  462.8 214.0 %reduce-scatter.2.cloned.1.call-start = ((), (), s32[]{:S(2)}) async-start(), calls=%async_computation.11 | async-start | bytes 4866048 | tf_op jit(solution)/shard_map/reduce_scatter | solution.py:244
  579.9 14.0 %copy-start.31 = (s32[32]{0:T(128)S(1)}, s32[32]{0:T(128)}, u32[]{:S(2)}) copy-start(s32[32]{0:T(128)} %param.35) | copy-start | bytes 388
  579.9 42.4 %copy-start.26 = (f32[2,3072]{1,0:T(2,128)S(1)}, f32[2,3072]{1,0:T(2,128)}, u32[]{:S(2)}) copy-start(f32[2,3072]{1,0:T(2,128)} %get-tuple-element.2887) | copy-start | bytes 73732
  579.9 42.4 %all-to-all-start.7 = ((bf16[32,8,4608]{2,1,0:T(8,128)(2,1)}), bf16[32,8,4608]{2,1,0:T(8,128)(2,1)S(1)}, u32[]{:S(2)}, u32[]{:S(2)}) async-start(bf16[32,8,4608]{2,1,0:T(8,128)(2,1)} %reshape_squeeze.39), calls=%async_computation.8 | async-start | bytes 4718592 | tf_op jit(solution)/shard_map/all_to_all | solution.py:39
  622.9 15.3 %all-to-all-start.4 = ((f32[4,2,3072]{2,1,0:T(2,128)}), f32[4,2,3072]{2,1,0:T(2,128)S(1)}, u32[]{:S(2)}, u32[]{:S(2)}) async-start(f32[4,2,3072]{2,1,0:T(2,128)} %broadcast_in_dim.133), calls=%async_computation.4 | async-start | bytes 196608 | tf_op jit(solution)/shard_map/all_to_all | solution.py:14
  638.2 36.1 %all-to-all-start.8 = ((bf16[32,8,4608]{2,1,0:T(8,128)(2,1)}), bf16[32,8,4608]{2,1,0:T(8,128)(2,1)S(1)}, u32[]{:S(2)}, u32[]{:S(2)}) async-start(bf16[32,8,4608]{2,1,0:T(8,128)(2,1)} %broadcast_select_fusion), calls=%async_computation.9 | async-start | bytes 4718592 | tf_op jit(solution)/shard_map/all_to_all | solution.py:41
  676.8 25.1 %all-to-all-start.5 = ((f32[384,4,24]{0,2,1:T(8,128)}), f32[384,4,24]{0,2,1:T(8,128)S(1)}, u32[]{:S(2)}, u32[]{:S(2)}) async-start(f32[384,4,24]{0,2,1:T(8,128)} %bitcast.308), calls=%async_computation.6 | async-start | bytes 294912 | tf_op jit(solution)/shard_map/all_to_all | solution.py:245
  (22 other events, 28.8 us)
Sparse Core Ops, SparseCore 0:
  272.5 83.3 all-gather.1
  474.1 177.7 reduce-scatter.1
where the time goes:
time: 720 us; the launch traced here: 710 us
  waiting for transfers between devices  334 us (46%)
  local copies, waits for them, and re-layouts  144 us (20%)
  matrix products  70.4 us (10%)
  starting transfers between devices  70.2 us (10%)
  other arithmetic  47.2 us (7%)
  blocking collectives  24 us (3%)
  between operations  17.9 us (2%)
    all_to_all x1, waiting for transfers between devices, body(): lax.all_to_all(grad_heads, 'seq', split_axis=1, concat_axis=3, tiled=True)  96.9 us
    all_gather x1, waiting for transfers between devices, body(): portion = lax.all_gather(scaled, 'seq', axis=1, tiled=True)  76.6 us
    all_to_all x1, waiting for transfers between devices, to_heads(): lax.all_to_all(parted, 'seq', split_axis=3, concat_axis=1, tiled=True)  49.8 us
    all_to_all x1, waiting for transfers between devices, move_in(): lax.all_to_all(portions, 'dp', split_axis=0, concat_axis=0, tiled=True)  30.6 us
    all_to_all x1, waiting for transfers between devices, move_out(): lax.all_to_all(portions, 'dp', split_axis=0, concat_axis=0, tiled=True)  28.4 us
    all_to_all x1, waiting for transfers between devices, move_in(): lax.all_to_all(arranged, 'dp', split_axis=0, concat_axis=0, tiled=True)  25.9 us
    all_to_all x1, waiting for transfers between devices, move_out(): lax.all_to_all(arranged, 'dp', split_axis=0, concat_axis=0, tiled=True)  25 us
    all_to_all x1, blocking collectives, body(): lax.all_to_all(attn_heads, 'seq', split_axis=1, concat_axis=2, tiled=True)  24 us
  transfers between devices with their start and end apart: 10, of which 8 were waited for; matrix products, arithmetic and copies ran while one was open for 8% of the time, Pallas kernels for 0%

commit v1 on v0

--- a/solution.py
+++ b/solution.py
@@ -1,3 +1,4 @@
+import functools
 import jax
 import jax.numpy as jnp
 from jax import lax
@@ -7,6 +8,15 @@
 TXT = 256
 BLOCK = 512
 NEGATIVE = -1e30
+
+
+def wait_the_chains(vec, out_dim):
+    return jnp.concatenate(
+        lax.all_to_all(jnp.stack(lax.psum(1, "seq") * [vec]), "seq", 0, 0), axis=out_dim
+    )
+
+
+_find_sources_all = functools.partial(wait_the_chains, out_dim=1)
 
 
 def from_everyone(x, axis):
@@ -235,7 +245,7 @@
     scaled = (cotangent.astype(jnp.float32) * gate[:, None, :]).astype(jnp.bfloat16)
     weight_rows = lax.dynamic_slice_in_dim(out_weight, seq_index * local_width, local_width, 0)
     flat_heads = attn_heads.reshape(2, seq_len, local_width)
-    portion = lax.all_gather(scaled, "seq", axis=1, tiled=True)
+    portion = _find_sources_all(scaled)
     weight_part = jnp.einsum("cnh,cnd->hd", flat_heads, portion, preferred_element_type=jnp.float32)
     grad_rows = jnp.einsum(
         "cnd,hd->cnh", portion, weight_rows, preferred_element_type=jnp.float32

time: 720 us -> 796 us (1.11)
  waiting for transfers between devices: 334 us -> 394 us
  local copies, waits for them, and re-layouts: 144 us -> 162 us
    all_to_all x0 -> x1, waiting for transfers between devices: none -> 133 us  [wait_the_chains(): lax.all_to_all(jnp.stack(lax.psum(1, 'seq') * [vec]), 'seq', 0, 0)]
    all_gather x1 -> x0, waiting for transfers between devices: 76.6 us -> none  [body(): portion = lax.all_gather(scaled, 'seq', axis=1, tiled=True)]
  transfers between devices with their start and end apart: 10 -> 10, of which waited for: 8 -> 8; matrix products, arithmetic and copies ran while one was open for 8% -> 7% of each run, Pallas kernels for 0% -> 0%
where the time goes in v1:
time: 796 us; the launch traced here: 785 us
  waiting for transfers between devices  394 us (49%)
  local copies, waits for them, and re-layouts  162 us (20%)
  starting transfers between devices  72.1 us (9%)
  matrix products  65.2 us (8%)
  other arithmetic  46.1 us (6%)
  blocking collectives  25.1 us (3%)
  between operations  18.2 us (2%)
    all_to_all x1, waiting for transfers between devices, wait_the_chains(): lax.all_to_all(jnp.stack(lax.psum(1, 'seq') * [vec]), 'seq', 0, 0)  133 us
    all_to_all x1, waiting for transfers between devices, body(): lax.all_to_all(grad_heads, 'seq', split_axis=1, concat_axis=3, tiled=True)  100 us
    all_to_all x1, waiting for transfers between devices, to_heads(): lax.all_to_all(parted, 'seq', split_axis=3, concat_axis=1, tiled=True)  49.8 us
    all_to_all x1, waiting for transfers between devices, move_in(): lax.all_to_all(portions, 'dp', split_axis=0, concat_axis=0, tiled=True)  30.6 us
    all_to_all x1, waiting for transfers between devices, move_out(): lax.all_to_all(portions, 'dp', split_axis=0, concat_axis=0, tiled=True)  27.7 us
    all_to_all x1, waiting for transfers between devices, move_out(): lax.all_to_all(arranged, 'dp', split_axis=0, concat_axis=0, tiled=True)  25.9 us
    all_to_all x1, waiting for transfers between devices, move_in(): lax.all_to_all(arranged, 'dp', split_axis=0, concat_axis=0, tiled=True)  25.9 us
    all_to_all x1, blocking collectives, body(): lax.all_to_all(attn_heads, 'seq', split_axis=1, concat_axis=2, tiled=True)  25.1 us
  transfers between devices with their start and end apart: 10, of which 8 were waited for; matrix products, arithmetic and copies ran while one was open for 7% of the time, Pallas kernels for 0%

profile of v1, /device:TPU:1, one launch (start us, length us, event | category | flops | bytes accessed | tf_op | source)
XLA Modules:
  0.0 784.7 jit_solution(17254479885756078074)
XLA Ops:
  12.0 9.3 %all-to-all-start = ((bf16[32,8,4608]{2,1,0:T(8,128)(2,1)}), bf16[32,8,4608]{2,1,0:T(8,128)(2,1)S(1)}, u32[]{:S(2)}, u32[]{:S(2)}) async-start(bf16[32,8,4608]{2,1,0:T(8,128)(2,1)} %get-tuple-element.2898), calls=%async_computation | async-start | bytes 4718592 | tf_op jit(solution)/shard_map/all_to_all | solution.py:40
  21.5 30.6 %all-to-all-done = bf16[32,8,4608]{2,1,0:T(8,128)(2,1)S(1)} async-done(((bf16[32,8,4608]{2,1,0:T(8,128)(2,1)}), bf16[32,8,4608]{2,1,0:T(8,128)(2,1)S(1)}, u32[]{:S(2)}, u32[]{:S(2)}) %all-to-all-start) | async-done | bytes 2359328 | tf_op jit(solution)/shard_map/all_to_all | solution.py:40
  66.1 25.9 %all-to-all-done.1 = bf16[32,8,4608]{2,1,0:T(8,128)(2,1)S(1)} async-done(((bf16[32,8,4608]{2,1,0:T(8,128)(2,1)}), bf16[32,8,4608]{2,1,0:T(8,128)(2,1)S(1)}, u32[]{:S(2)}, u32[]{:S(2)}) %all-to-all-start.1) | async-done | bytes 2359328 | tf_op jit(solution)/shard_map/all_to_all | solution.py:42
  104.3 8.3 %all-to-all-start.2 = ((bf16[2,256,3,4,384]{1,4,2,0,3:T(8,128)(2,1)}), bf16[2,256,3,4,384]{1,4,2,0,3:T(8,128)(2,1)}, u32[]{:S(2)}, u32[]{:S(2)}) async-start(bf16[2,256,3,4,384]{1,4,2,0,3:T(8,128)(2,1)} %copy.336), calls=%async_computation.2 | async-start | bytes 9437184 | tf_op jit(solution)/shard_map/all_to_all | solution.py:59
  117.1 49.8 %all-to-all-done.2 = bf16[2,256,3,4,384]{1,4,2,0,3:T(8,128)(2,1)} async-done(((bf16[2,256,3,4,384]{1,4,2,0,3:T(8,128)(2,1)}), bf16[2,256,3,4,384]{1,4,2,0,3:T(8,128)(2,1)}, u32[]{:S(2)}, u32[]{:S(2)}) %all-to-all-start.2) | async-done | bytes 4718624 | tf_op jit(solution)/shard_map/all_to_all | solution.py:59
  166.9 6.6 copy.337
  181.5 26.0 %while.235 = (s32[]{:T(128)}, bf16[1024,3,128]{0,2,1:T(8,128)(2,1)S(1)}, f32[3,1024]{1,0:T(4,128)}, s32[]{:T(128)}, bf16[1024,3,128]{2,0,1:T(8,128)(2,1)}, /*ind...) while((s32[]{:T(128)}, ...), condition=%wide.region_16.18_spmd, body=%wide.region_9.17_spmd.sunk | while | flops 613564928 | bytes 14026645 | solution.py:128
  187.9 6.5 while.243
  201.0 6.5 while.243
  218.4 8.0 %while.232 = (s32[]{:T(128)}, bf16[1024,3,128]{0,2,1:T(8,128)(2,1)S(1)}, f32[3,1024]{1,0:T(4,128)}, s32[]{:T(128)}, bf16[1024,3,128]{2,0,1:T(8,128)(2,1)}, /*ind...) while((s32[]{:T(128)}, ...), condition=%wide.region_8.10_spmd, body=%wide.region_1.9_spmd.sunk | while | flops 613564928 | bytes 14026645 | solution.py:128
  234.4 25.1 %all_to_all.94 = bf16[2,1024,1,384]{3,0,2,1:T(2,128)(2,1)S(1)} all-to-all(bf16[2,1024,1,384]{3,0,2,1:T(2,128)(2,1)} %copy.348), channel_id=1, replica_groups=mesh['dp'=32,'seq'=4] {'seq'}, dimensions={1} | all-to-all | bytes 3145728 | tf_op jit(solution)/shard_map/all_to_all | solution.py:239
  262.4 11.0 %fusion.166 = (f32[2,3072]{1,0:T(2,128)}, bf16[2,256,3072]{2,1,0:T(8,128)(2,1)}, bf16[2,256,3072]{2,1,0:T(8,128)(2,1)}) fusion(bf16[2,256,3072]{2,1,0:T(8,128)(2,1)} %param.31, f32[2,3072]{1,0:T(2,128)S(1)} %copy-done.33, bf16[2,256,1536]{2,1,0:T(8,128)(2,1)} %reshape.324, bf16[1536,3072]{1,0:T(8,128)(2,1)} %param.32), kind=kOutput, calls=%fused_computation.198 | convolution fusion | flops 4842842112 | bytes 20496384 | tf_op jit(solution)/shard_map/crh,hd->crd/dot_general | solution.py:242
  278.0 7.3 stack.56
  285.3 7.6 all-to-all-start.5
  298.8 132.8 %all-to-all-done.5 = bf16[4,2,256,3072]{2,3,1,0:T(8,128)(2,1)} async-done(((bf16[4,2,256,3072]{2,3,1,0:T(8,128)(2,1)}), bf16[4,2,256,3072]{2,3,1,0:T(8,128)(2,1)}, u32[]{:S(2)}, u32[]{:S(2)}) %all-to-all-start.5) | async-done | bytes 12582944 | tf_op jit(solution)/shard_map/all_to_all | solution.py:15
  431.5 6.6 copy.407
  438.1 7.7 fusion.171
  450.5 36.2 %while.239 = (s32[]{:T(128)}, f32[1024,3,128]{0,2,1:T(8,128)}, f32[1024,3,128]{2,0,1:T(8,128)S(1)}, f32[1024,3,128]{2,0,1:T(8,128)}, s32[]{:T(128)}, /*index=5*/...) while((s32[]{:T(128)}, f32[1024,3,128]{0,2,1:T(8,128)}, ...), condition=%wide.region_27.29_spmd, body=%wide.region_24.28_spmd.sunk | while | flops 1015355392 | bytes 44485404 | solution.py:189
  454.3 13.4 %while.245 = (s32[]{:T(128)}, f32[512,3,128]{0,2,1:T(8,128)S(1)}, f32[1024,3,128]{2,0,1:T(8,128)S(1)}, f32[1024,3,128]{2,0,1:T(8,128)}, s32[]{:T(128)}, /*index=...) while((s32[]{:T(128)}, f32[512,3,128]{0,2,1:T(8,128)S(1)}, ...), condition=%wide.region_26.27_spmd.clone.clone, body=%wide.region_25.26_spmd.clone.clone.sunk | while | flops 1015355392 | bytes 39741808 | solution.py:184
  472.4 13.4 %while.245 = (s32[]{:T(128)}, f32[512,3,128]{0,2,1:T(8,128)S(1)}, f32[1024,3,128]{2,0,1:T(8,128)S(1)}, f32[1024,3,128]{2,0,1:T(8,128)}, s32[]{:T(128)}, /*index=...) while((s32[]{:T(128)}, f32[512,3,128]{0,2,1:T(8,128)S(1)}, ...), condition=%wide.region_26.27_spmd.clone.clone, body=%wide.region_25.26_spmd.clone.clone.sunk | while | flops 1015355392 | bytes 39741808 | solution.py:184
  498.2 11.7 %while.237 = (s32[]{:T(128)}, f32[1024,3,128]{0,2,1:T(8,128)}, f32[1024,3,128]{2,0,1:T(8,128)S(1)}, f32[1024,3,128]{2,0,1:T(8,128)}, s32[]{:T(128)}, /*index=5*/...) while((s32[]{:T(128)}, f32[1024,3,128]{0,2,1:T(8,128)}, ...), condition=%wide.region_23.25_spmd, body=%wide.region_20.24_spmd.sunk | while | flops 1015355392 | bytes 44485404 | solution.py:189
  502.2 6.8 while.244
  520.1 12.6 %copy.374 = bf16[2,1024,3,1,384]{4,0,3,2,1:T(2,128)(2,1)} copy(bf16[2,1024,3,1,384]{1,4,2,0,3:T(8,128)(2,1)} %maximum_bitcast_fusion) | data formatting | bytes 9437184 | tf_op jit(solution)/shard_map/reshape | solution.py:274
  539.0 11.9 %convolution_bitcast_fusion.4 = f32[384,3072]{0,1:T(8,128)} fusion(bf16[2,1024,3072]{1,2,0:T(8,128)(2,1)} %bitcast.291, bf16[1,1024,384]{2,1,0:T(8,128)(2,1)S(1)} %copy-done.26, bf16[1,1024,384]{2,1,0:T(8,128)(2,1)S(1)} %copy-done.27), kind=kOutput, calls=%fused_computation.204 | convolution fusion | flops 4832624640 | bytes 18874368 | tf_op jit(solution)/shard_map/cnh,cnd->hd/dot_general | solution.py:249
  550.9 100.3 %all-to-all-done.7 = bf16[2,1024,3,1,384]{4,0,3,2,1:T(2,128)(2,1)} async-done(((bf16[2,1024,3,1,384]{4,0,3,2,1:T(2,128)(2,1)}), bf16[2,1024,3,1,384]{4,0,3,2,1:T(2,128)(2,1)}, u32[]{:S(2)}, u32[]{:S(2)}) %all-to-all-start.7) | async-done | bytes 4718624 | tf_op jit(solution)/shard_map/all_to_all | solution.py:275
  660.3 8.9 %all-to-all-start.8 = ((bf16[32,8,4608]{2,1,0:T(8,128)(2,1)}), bf16[32,8,4608]{2,1,0:T(8,128)(2,1)S(1)}, u32[]{:S(2)}, u32[]{:S(2)}) async-start(bf16[32,8,4608]{2,1,0:T(8,128)(2,1)} %reshape_squeeze.39), calls=%async_computation.9 | async-start | bytes 4718592 | tf_op jit(solution)/shard_map/all_to_all | solution.py:49
  669.2 27.7 %all-to-all-done.8 = bf16[32,8,4608]{2,1,0:T(8,128)(2,1)S(1)} async-done(((bf16[32,8,4608]{2,1,0:T(8,128)(2,1)}), bf16[32,8,4608]{2,1,0:T(8,128)(2,1)S(1)}, u32[]{:S(2)}, u32[]{:S(2)}) %all-to-all-start.8) | async-done | bytes 2359328 | tf_op jit(solution)/shard_map/all_to_all | solution.py:49
  697.6 9.2 %all-to-all-start.4 = ((f32[4,2,3072]{2,1,0:T(2,128)}), f32[4,2,3072]{2,1,0:T(2,128)S(1)}, u32[]{:S(2)}, u32[]{:S(2)}) async-start(f32[4,2,3072]{2,1,0:T(2,128)} %broadcast_in_dim.133), calls=%async_computation.4 | async-start | bytes 196608 | tf_op jit(solution)/shard_map/all_to_all | solution.py:24
  713.4 6.6 all-to-all-start.9
  724.9 25.9 %all-to-all-done.9 = bf16[32,8,4608]{2,1,0:T(8,128)(2,1)S(1)} async-done(((bf16[32,8,4608]{2,1,0:T(8,128)(2,1)}), bf16[32,8,4608]{2,1,0:T(8,128)(2,1)S(1)}, u32[]{:S(2)}, u32[]{:S(2)}) %all-to-all-start.9) | async-done | bytes 2359328 | tf_op jit(solution)/shard_map/all_to_all | solution.py:51
  753.4 11.8 %all-to-all-start.6 = ((f32[384,4,24]{0,2,1:T(8,128)}), f32[384,4,24]{0,2,1:T(8,128)S(1)}, u32[]{:S(2)}, u32[]{:S(2)}) async-start(f32[384,4,24]{0,2,1:T(8,128)} %bitcast.313), calls=%async_computation.7 | async-start | bytes 294912 | tf_op jit(solution)/shard_map/all_to_all | solution.py:255
  770.1 6.6 copy.379
  (302 shorter events, 229.5 us)
Async XLA Ops:
  12.0 9.4 %copy-start.34 = (s32[32]{0:T(128)S(1)}, s32[32]{0:T(128)}, u32[]{:S(2)}) copy-start(s32[32]{0:T(128)} %param.35) | copy-start | bytes 388
  12.0 40.1 %all-to-all-start = ((bf16[32,8,4608]{2,1,0:T(8,128)(2,1)}), bf16[32,8,4608]{2,1,0:T(8,128)(2,1)S(1)}, u32[]{:S(2)}, u32[]{:S(2)}) async-start(bf16[32,8,4608]{2,1,0:T(8,128)(2,1)} %get-tuple-element.2898), calls=%async_computation | async-start | bytes 4718592 | tf_op jit(solution)/shard_map/all_to_all | solution.py:40
  57.6 34.4 %all-to-all-start.1 = ((bf16[32,8,4608]{2,1,0:T(8,128)(2,1)}), bf16[32,8,4608]{2,1,0:T(8,128)(2,1)S(1)}, u32[]{:S(2)}, u32[]{:S(2)}) async-start(bf16[32,8,4608]{2,1,0:T(8,128)(2,1)} %broadcast_select_fusion.1), calls=%async_computation.1 | async-start | bytes 4718592 | tf_op jit(solution)/shard_map/all_to_all | solution.py:42
  94.1 5.5 copy-start.13
  104.3 9.5 %copy-start.31 = (s32[64]{0:T(128)S(1)}, s32[64]{0:T(128)}, u32[]{:S(2)}) copy-start(s32[64]{0:T(128)} %param.34) | copy-start | bytes 772
  104.3 9.5 %copy-start.32 = (s32[64]{0:T(128)S(1)}, s32[64]{0:T(128)}, u32[]{:S(2)}) copy-start(s32[64]{0:T(128)} %param.33) | copy-start | bytes 772
  104.3 62.6 %all-to-all-start.2 = ((bf16[2,256,3,4,384]{1,4,2,0,3:T(8,128)(2,1)}), bf16[2,256,3,4,384]{1,4,2,0,3:T(8,128)(2,1)}, u32[]{:S(2)}, u32[]{:S(2)}) async-start(bf16[2,256,3,4,384]{1,4,2,0,3:T(8,128)(2,1)} %copy.336), calls=%async_computation.2 | async-start | bytes 9437184 | tf_op jit(solution)/shard_map/all_to_all | solution.py:59
  207.5 7.5 copy-start
  207.5 7.5 copy-start.9
  210.4 6.2 copy-start.20
  226.4 7.9 %copy-start.2 = (bf16[1024,3,128]{2,0,1:T(8,128)(2,1)}, bf16[1024,3,128]{2,0,1:T(8,128)(2,1)S(1)}, u32[]{:S(2)}) copy-start(bf16[1024,3,128]{2,0,1:T(8,128)(2,1)S(1)} %get-tuple-element.4366) | copy-start | bytes 2359300
  226.4 71.2 %copy-start.7 = (bf16[1024,3,128]{0,2,1:T(8,128)(2,1)}, bf16[1024,3,128]{0,2,1:T(8,128)(2,1)S(1)}, u32[]{:S(2)}) copy-start(bf16[1024,3,128]{0,2,1:T(8,128)(2,1)S(1)} %get-tuple-element.1855) | copy-start | bytes 2359300
  285.3 7.6 copy-start.21
  285.3 146.2 %all-to-all-start.5 = ((bf16[4,2,256,3072]{2,3,1,0:T(8,128)(2,1)}), bf16[4,2,256,3072]{2,3,1,0:T(8,128)(2,1)}, u32[]{:S(2)}, u32[]{:S(2)}) async-start(bf16[4,2,256,3072]{2,3,1,0:T(8,128)(2,1)} %stack.56), calls=%async_computation.5 | async-start | bytes 25165824 | tf_op jit(solution)/shard_map/all_to_all | solution.py:15
  292.9 3.5 copy-start.10
  438.1 7.7 copy-start.6
  447.8 2.7 copy-start.1
  489.3 4.2 copy-start.14
  490.9 3.6 copy-start.4
  490.9 3.6 copy-start.8
  495.5 2.7 copy-start.3
  512.4 3.3 copy-start.17
  532.8 6.3 copy-start.26
  532.8 6.3 copy-start.27
  532.8 118.5 %all-to-all-start.7 = ((bf16[2,1024,3,1,384]{4,0,3,2,1:T(2,128)(2,1)}), bf16[2,1024,3,1,384]{4,0,3,2,1:T(2,128)(2,1)}, u32[]{:S(2)}, u32[]{:S(2)}) async-start(bf16[2,1024,3,1,384]{4,0,3,2,1:T(2,128)(2,1)} %copy.374), calls=%async_computation.8 | async-start | bytes 9437184 | tf_op jit(solution)/shard_map/all_to_all | solution.py:275
  538.8 214.6 %reduce-scatter.2.cloned.1.call-start = ((), (), s32[]{:S(2)}) async-start(), calls=%async_computation.11 | async-start | bytes 4866048 | tf_op jit(solution)/shard_map/reduce_scatter | solution.py:254
  660.3 8.9 %copy-start.35 = (s32[32]{0:T(128)S(1)}, s32[32]{0:T(128)}, u32[]{:S(2)}) copy-start(s32[32]{0:T(128)} %param.35) | copy-start | bytes 388
  660.3 36.6 %copy-start.30 = (f32[2,3072]{1,0:T(2,128)S(1)}, f32[2,3072]{1,0:T(2,128)}, u32[]{:S(2)}) copy-start(f32[2,3072]{1,0:T(2,128)} %get-tuple-element.2887) | copy-start | bytes 73732
  660.3 36.6 %all-to-all-start.8 = ((bf16[32,8,4608]{2,1,0:T(8,128)(2,1)}), bf16[32,8,4608]{2,1,0:T(8,128)(2,1)S(1)}, u32[]{:S(2)}, u32[]{:S(2)}) async-start(bf16[32,8,4608]{2,1,0:T(8,128)(2,1)} %reshape_squeeze.39), calls=%async_computation.9 | async-start | bytes 4718592 | tf_op jit(solution)/shard_map/all_to_all | solution.py:49
  697.6 15.8 %all-to-all-start.4 = ((f32[4,2,3072]{2,1,0:T(2,128)}), f32[4,2,3072]{2,1,0:T(2,128)S(1)}, u32[]{:S(2)}, u32[]{:S(2)}) async-start(f32[4,2,3072]{2,1,0:T(2,128)} %broadcast_in_dim.133), calls=%async_computation.4 | async-start | bytes 196608 | tf_op jit(solution)/shard_map/all_to_all | solution.py:24
  713.4 37.5 %all-to-all-start.9 = ((bf16[32,8,4608]{2,1,0:T(8,128)(2,1)}), bf16[32,8,4608]{2,1,0:T(8,128)(2,1)S(1)}, u32[]{:S(2)}, u32[]{:S(2)}) async-start(bf16[32,8,4608]{2,1,0:T(8,128)(2,1)} %broadcast_select_fusion), calls=%async_computation.10 | async-start | bytes 4718592 | tf_op jit(solution)/shard_map/all_to_all | solution.py:51
  753.4 23.4 %all-to-all-start.6 = ((f32[384,4,24]{0,2,1:T(8,128)}), f32[384,4,24]{0,2,1:T(8,128)S(1)}, u32[]{:S(2)}, u32[]{:S(2)}) async-start(f32[384,4,24]{0,2,1:T(8,128)} %bitcast.313), calls=%async_computation.7 | async-start | bytes 294912 | tf_op jit(solution)/shard_map/all_to_all | solution.py:255
  (26 other events, 38.0 us)
Sparse Core Ops, SparseCore 0:
  551.1 172.5 reduce-scatter.1
